TPU v7x, 32 devices: a whole 2x2x4 slice. The times are simulated.
32 devices in a mesh: mem: 8 (over y, x, core), pix: 4 (over z).
Axes of the slice: x: 2, y: 2, z: 4, core: 2. Of those that a mesh axis runs over, the one named last changes fastest.
Arguments:
- prior_motion: bfloat16 [64, 16, 131072], P('mem', None, 'pix'), may hold values from -6 to 6
- measured_motion: float32 [1200], replicated, may hold values from -1.6 to 1.6
- measurement_noise_stddev: float32 [1200], replicated, may hold values from 0.05 to 0.5
- gaussian_jitter: float32 [2, 1200, 64], replicated, may hold values from -6 to 6
- scene_couples: int32 [2, 1200], replicated, may hold values from 0 to 15, as said below
- targeted_tile_number: int32 [1200], replicated, may hold values from 0 to 2047
Outputs:
- analysis: bfloat16 [64, 16, 131072], P('mem', None, 'pix')
Inputs may be any that keep to these rules, and one draw needn't show every extreme that they name: scene_couples[0, k] < scene_couples[1, k]: row 0 holds the earlier acquisition, row 1 the later.
All inputs are finite; a program needn't handle non-finite values.
Results may differ from a plain program's by a relative error of at most 0.011.
Values may be sent and summed in bfloat16 or wider, within the bound.
A program may use at most 192 MiB of HBM per device.

v0:
```python
import math
import jax
import jax.numpy as jnp
from jax import lax
from jax.sharding import PartitionSpec as P

BLK = 64
PASS_COUNT = 2


def block_sums(pieces):
    part_cells = pieces.shape[2]
    block_count = part_cells // BLK
    summer = (
        jnp.arange(part_cells, dtype=jnp.int32)[:, None] // BLK
        == jnp.arange(block_count, dtype=jnp.int32)[None, :]
    ).astype(jnp.bfloat16)
    flat = jnp.dot(pieces.reshape(-1, part_cells), summer, preferred_element_type=jnp.float32)
    return flat.reshape(pieces.shape[0], pieces.shape[1], block_count)


def with_sums(pieces):
    return (pieces, block_sums(pieces))


def to_pixels(ground_motion_vector):
    return with_sums(
        lax.all_to_all(ground_motion_vector, "mem", split_axis=2, concat_axis=0, tiled=True)
    )


def to_members(pixel_state):
    return lax.all_to_all(pixel_state, "mem", split_axis=0, concat_axis=2, tiled=True)


def predict(sums, picker):
    flat_sums = sums.reshape(sums.shape[0], -1)
    return (
        jnp.dot(
            picker, flat_sums.T, precision=lax.Precision.HIGHEST, preferred_element_type=jnp.float32
        )
        / BLK
    )


def member_terms(predicted, measured_motion, member_anomaly, noise):
    realization_vectors = predicted.shape[1]
    centred = predicted - jnp.mean(predicted, axis=1, keepdims=True)
    scaled = centred / (member_anomaly[:, None] * math.sqrt(realization_vectors - 1))
    misfit = (
        measured_motion[:, None] + member_anomaly[:, None] * noise - predicted
    ) / member_anomaly[:, None]
    return (scaled, misfit)


def products(scaled, misfit):
    gram = jnp.dot(
        scaled.T, scaled, precision=lax.Precision.HIGHEST, preferred_element_type=jnp.float32
    )
    cross = jnp.dot(
        scaled.T, misfit, precision=lax.Precision.HIGHEST, preferred_element_type=jnp.float32
    )
    return (gram, cross)


def solve_mixing(gram, cross):
    realization_vectors = gram.shape[0]
    factor = jnp.linalg.cholesky(jnp.eye(realization_vectors, dtype=jnp.float32) + gram)
    return (
        jax.scipy.linalg.cho_solve((factor, True), cross) / math.sqrt(realization_vectors - 1)
    ).astype(jnp.bfloat16)


def update(pixel_state, mixing):
    realization_vectors = pixel_state.shape[0]
    average = jnp.sum(pixel_state, axis=0, dtype=jnp.float32) / realization_vectors
    anomaly = (pixel_state.astype(jnp.float32) - average).astype(jnp.bfloat16)
    change = jnp.dot(
        mixing.T, anomaly.reshape(realization_vectors, -1), preferred_element_type=jnp.float32
    )
    return (pixel_state.astype(jnp.float32) + change.reshape(pixel_state.shape)).astype(
        jnp.bfloat16
    )


def body(
    prior_motion,
    measured_motion,
    measurement_noise_stddev,
    gaussian_jitter,
    scene_couples,
    targeted_tile_number,
):
    cells_per_tile = prior_motion.shape[2]
    part_width = cells_per_tile // lax.axis_size("mem")
    local_blocks = part_width // BLK
    first_block = (
        lax.axis_index("pix") * cells_per_tile + lax.axis_index("mem") * part_width
    ) // BLK
    block_range = first_block + jnp.arange(local_blocks, dtype=jnp.int32)
    block_table = (targeted_tile_number[:, None] == block_range[None, :]).astype(jnp.float32)
    scene_timeline = jnp.arange(prior_motion.shape[1], dtype=jnp.int32)
    pair_table = (scene_timeline[None, :] == scene_couples[1][:, None]).astype(jnp.float32) - (
        scene_timeline[None, :] == scene_couples[0][:, None]
    ).astype(jnp.float32)
    picker = (pair_table[:, :, None] * block_table[:, None, :]).reshape(pair_table.shape[0], -1)
    member_anomaly = jnp.sqrt(jnp.float32(float(PASS_COUNT))) * measurement_noise_stddev
    pixel_state, sums = to_pixels(prior_motion)
    for iteration in range(PASS_COUNT):
        if iteration > 0:
            sums = block_sums(pixel_state)
        predicted = predict(sums, picker)
        predicted = lax.psum(predicted, ("mem", "pix"))
        scaled, misfit = member_terms(
            predicted, measured_motion, member_anomaly, gaussian_jitter[iteration]
        )
        gram, cross = products(scaled, misfit)
        pixel_state = update(pixel_state, solve_mixing(gram, cross))
    return to_members(pixel_state)


def solution(mesh):
    return jax.shard_map(
        body,
        mesh=mesh,
        in_specs=(P("mem", None, "pix"), P(), P(), P(), P(), P()),
        out_specs=P("mem", None, "pix"),
        check_vma=False,
    )
```

profile of v0, /device:TPU:8, one launch (start us, length us, event | category | flops | bytes accessed | tf_op | source)
XLA Modules:
  0.0 957.3 jit_solution(7385386645052010220)
XLA Ops:
  6.5 52.6 %copy.41 = bf16[8,16,32768]{1,0,2:T(8,128)(2,1)} copy(bf16[8,16,32768]{2,1,0:T(8,128)(2,1)} %param.9) | data formatting | bytes 16777216 | tf_op args[0]
  59.1 103.9 %reshape.195 = bf16[8,2,262144]{2,1,0:T(2,128)(2,1)} reshape(bf16[32768,8,16]{2,1,0:T(8,128)(2,1)} %bitcast.86) | data formatting | bytes 16777216
  171.8 90.4 %all-to-all-done = bf16[8,2,262144]{2,1,0:T(2,128)(2,1)} async-done(((bf16[8,2,262144]{2,1,0:T(2,128)(2,1)}), bf16[8,2,262144]{2,1,0:T(2,128)(2,1)}, u32[]{:S(2)}, u32[]{:S(2)}) %all-to-all-start) | async-done | bytes 8388640 | tf_op jit(solution)/shard_map/all_to_all | solution.py:28
  262.2 80.3 %reshape.196 = bf16[32768,8,16]{2,1,0:T(8,128)(2,1)} reshape(bf16[8,2,262144]{2,1,0:T(2,128)(2,1)} %all-to-all-done) | data formatting | bytes 16777216
  342.5 52.2 %copy.65 = bf16[8,16,8,4096]{3,2,1,0:T(8,128)(2,1)} copy(bf16[8,16,8,4096]{1,0,3,2:T(8,128)(2,1)} %bitcast) | data formatting | bytes 16777216 | tf_op jit(solution)/shard_map/all_to_all | solution.py:28
  394.7 11.4 %bitcast_convert_fusion = f32[8,8,16,4096]{3,0,2,1:T(8,128)} fusion(bf16[8,16,8,4096]{3,2,1,0:T(8,128)(2,1)} %copy.65), kind=kLoop, calls=%fused_computation.14 | loop fusion | flops 4194304 | bytes 25165824 | tf_op jit(solution)/shard_map/convert_element_type | solution.py:81
  406.1 5.2 fusion.8
  411.3 60.0 %copy.44 = bf16[8,8,16,4096]{3,2,1,0:T(8,128)(2,1)} copy(bf16[8,8,16,4096]{2,1,3,0:T(8,128)(2,1)} %bitcast.4) | data formatting | bytes 16777216 | tf_op jit(solution)/shard_map/all_to_all | solution.py:28
  471.3 6.5 convolution_bitcast_fusion
  478.2 6.6 convolution_multiply_fusion.1
  484.9 15.2 %copy.90 = f32[8,8,16,4096]{3,2,1,0:T(8,128)S(1)} copy(f32[8,8,16,4096]{3,0,2,1:T(8,128)} %bitcast_convert_fusion) | data formatting | bytes 33554432 | tf_op jit(solution)/shard_map/convert_element_type | solution.py:81
  500.1 10.9 %copy.73 = f32[8,8,16,4096]{3,1,2,0:T(8,128)S(1)} copy(f32[8,8,16,4096]{3,2,1,0:T(8,128)S(1)} %copy.90) | data formatting | bytes 33554432
  515.0 98.2 %all-reduce.3.cloned.1.call-done = f32[1200,64]{0,1:T(8,128)} async-done(((f32[1200,64]{0,1:T(8,128)}), f32[1200,64]{0,1:T(8,128)}) %all-reduce.3.cloned.1.call-update) | async-done | bytes 307216 | tf_op jit(solution)/shard_map/psum | solution.py:113
  615.9 5.8 cholesky.44
  630.1 21.8 %convert_reduce_fusion = (f32[16,4096]{1,0:T(8,128)S(1)}, bf16[64,16,4096]{2,0,1:T(8,128)(2,1)}) fusion(bf16[64,64,1]{1,0,2:T(8,128)(2,1)S(1)} %fusion.14, bf16[8,16,8,4096]{3,2,1,0:T(8,128)(2,1)} %bitcast.113, f32[8,8,16,4096]{3,0,2,1:T(8,128)} %bitcast_convert_fusion), kind=kOutput, calls=%fused_computation.2 | convolution fusion | flops 553582592 | bytes 33824768 | tf_op jit(solution)/shard_map/dot_general | solution.py:78
  651.9 11.4 %copy.51 = bf16[64,16,4096]{2,1,0:T(8,128)(2,1)} copy(bf16[64,16,4096]{2,0,1:T(8,128)(2,1)} %get-tuple-element.12) | data formatting | bytes 16777216 | tf_op jit(solution)/shard_map/convert_element_type | solution.py:81
  663.2 5.8 fusion.9
  669.2 6.6 convolution_multiply_fusion
  675.9 128.1 %all-reduce.5.cloned.1.call-done = f32[1200,64]{0,1:T(8,128)} async-done(((f32[1200,64]{0,1:T(8,128)}), f32[1200,64]{0,1:T(8,128)}) %all-reduce.5.cloned.1.call-update) | async-done | bytes 307216 | tf_op jit(solution)/shard_map/psum | solution.py:113
  806.6 5.8 cholesky.55
  820.8 10.6 %fusion.1 = bf16[64,16,4096]{2,0,1:T(8,128)(2,1)} fusion(bf16[64,16,4096]{2,0,1:T(8,128)(2,1)} %get-tuple-element.12, bf16[64,64,1]{1,0,2:T(8,128)(2,1)S(1)} %fusion.13, f32[16,4096]{1,0:T(8,128)S(1)} %broadcast_multiply_fusion.1), kind=kOutput, calls=%fused_computation.4 | convolution fusion | flops 562036736 | bytes 17047552 | tf_op jit(solution)/shard_map/dot_general | solution.py:78
  831.4 11.2 %copy.58 = bf16[64,16,4096]{2,1,0:T(8,128)(2,1)} copy(bf16[64,16,4096]{2,0,1:T(8,128)(2,1)} %fusion.1) | data formatting | bytes 16777216 | tf_op jit(solution)/shard_map/convert_element_type | solution.py:81
  842.6 99.7 %all_to_all.33 = bf16[64,16,4096]{2,1,0:T(8,128)(2,1)} all-to-all(bf16[64,16,4096]{2,1,0:T(8,128)(2,1)} %copy.58), channel_id=1, replica_groups=mesh['mem'=8,'pix'=4] {'mem'}, dimensions={0} | all-to-all | bytes 16777216 | tf_op jit(solution)/shard_map/all_to_all | solution.py:33
  942.3 7.9 copy.72
  (53 shorter events, 35.0 us)
Async XLA Ops:
  163.1 5.7 copy-start
  163.1 5.7 copy-start.1
  163.1 5.7 copy-start.2
  163.1 99.1 %all-to-all-start = ((bf16[8,2,262144]{2,1,0:T(2,128)(2,1)}), bf16[8,2,262144]{2,1,0:T(2,128)(2,1)}, u32[]{:S(2)}, u32[]{:S(2)}) async-start(bf16[8,2,262144]{2,1,0:T(2,128)(2,1)} %reshape.195), calls=%async_computation | async-start | bytes 16777216 | tf_op jit(solution)/shard_map/all_to_all | solution.py:28
  168.2 445.1 %all-reduce.3.cloned.1.call-start = ((), (), s32[]{:S(2)}) async-start(), calls=%async_computation.2 | async-start | bytes 655360 | tf_op jit(solution)/shard_map/psum | solution.py:113
  484.9 319.1 %all-reduce.5.cloned.1.call-start = ((), (), s32[]{:S(2)}) async-start(), calls=%async_computation.3 | async-start | bytes 655360 | tf_op jit(solution)/shard_map/psum | solution.py:113
  511.1 117.0 %copy-start.3 = (f32[2,1200,64]{1,2,0:T(8,128)S(1)}, f32[2,1200,64]{1,2,0:T(8,128)}, u32[]{:S(2)}) copy-start(f32[2,1200,64]{1,2,0:T(8,128)} %param.12) | copy-start | bytes 1843204
  511.1 117.0 %copy-start.4 = (f32[1200]{0:T(1024)S(1)}, f32[1200]{0:T(1024)}, u32[]{:S(2)}) copy-start(f32[1200]{0:T(1024)} %param.10) | copy-start | bytes 14404
Sparse Core Ops, SparseCore 0:
  485.0 128.2 all-reduce.2
  676.0 127.9 all-reduce.4
where the time goes:
time: 970 us; the launch traced here: 957 us
  local copies, waits for them, and re-layouts  406 us (42%)
  waiting for transfers between devices  317 us (33%)
  blocking collectives  99.7 us (10%)
  matrix products  64.9 us (7%)
  other arithmetic  49.9 us (5%)
  between operations  13.9 us (1%)
    unnamed x15, local copies, waits for them, and re-layouts  248 us
    psum x2, waiting for transfers between devices, body(): predicted = lax.psum(predicted, ('mem', 'pix'))  226 us
    all_to_all x2, local copies, waits for them, and re-layouts, to_pixels(): lax.all_to_all(ground_motion_vector, 'mem', split_axis=2, concat_axis=0,...  112 us
    all_to_all x1, blocking collectives, to_members(): lax.all_to_all(pixel_state, 'mem', split_axis=0, concat_axis=2, tiled=True)  99.7 us
    all_to_all x1, waiting for transfers between devices, to_pixels(): lax.all_to_all(ground_motion_vector, 'mem', split_axis=2, concat_axis=0,...  90.4 us
    dot_general x2, matrix products, update(): jnp.dot(mixing.T, anomaly.reshape(realization_vectors, -1), preferred_ele...  32.4 us
    convert_element_type x2, local copies, waits for them, and re-layouts, update(): (pixel_state.astype(jnp.float32) + change.reshape(pixel_state.shape)).ast...  22.6 us
  transfers between devices with their start and end apart: 3, of which 3 were waited for; matrix products, arithmetic and copies ran while one was open for 3% of the time, Pallas kernels for 0%

commit v1 on v0

--- a/solution.py
+++ b/solution.py
@@ -25,7 +25,15 @@
 
 def to_pixels(ground_motion_vector):
     return with_sums(
-        lax.all_to_all(ground_motion_vector, "mem", split_axis=2, concat_axis=0, tiled=True)
+        jnp.concatenate(
+            lax.all_to_all(
+                jnp.stack(jnp.split(ground_motion_vector, lax.axis_size("mem"), axis=2)),
+                "mem",
+                0,
+                0,
+            ),
+            axis=0,
+        )
     )
 
 

time: 970 us -> 621 us (0.64)
  local copies, waits for them, and re-layouts: 406 us -> 60.2 us
    unnamed x15 -> x19, local copies, waits for them, and re-layouts: 248 us -> 26.9 us
    all_to_all x2 -> x0, local copies, waits for them, and re-layouts: 112 us -> none  [to_pixels(): lax.all_to_all(ground_motion_vector, 'mem', split_axis=2, concat_axis=0,...]
    convert_element_type x1 -> x0, local copies, waits for them, and re-layouts: 15.2 us -> none  [update(): pixel_state.astype(jnp.float32) + change.reshape(pixel_state.shape)]
    convert_element_type x1 -> x0, other arithmetic: 11.4 us -> none  [update(): pixel_state.astype(jnp.float32) + change.reshape(pixel_state.shape)]
    unnamed x1 -> x2, other arithmetic: 0.02 us -> 10.9 us
  transfers between devices with their start and end apart: 3 -> 3, of which waited for: 3 -> 3; matrix products, arithmetic and copies ran while one was open for 3% -> 5% of each run, Pallas kernels for 0% -> 0%
where the time goes in v1:
time: 621 us; the launch traced here: 614 us
  waiting for transfers between devices  321 us (52%)
  blocking collectives  99.7 us (16%)
  matrix products  64 us (10%)
  local copies, waits for them, and re-layouts  60.2 us (10%)
  other arithmetic  48.9 us (8%)
  between operations  13.9 us (2%)
    psum x2, waiting for transfers between devices, body(): predicted = lax.psum(predicted, ('mem', 'pix'))  230 us
    all_to_all x1, blocking collectives, to_members(): lax.all_to_all(pixel_state, 'mem', split_axis=0, concat_axis=2, tiled=True)  99.7 us
    all_to_all x1, waiting for transfers between devices, to_pixels(): lax.all_to_all(jnp.stack(jnp.split(ground_motion_vector, lax.axis_size('m...  90.9 us
    dot_general x2, matrix products, update(): jnp.dot(mixing.T, anomaly.reshape(realization_vectors, -1), preferred_ele...  32.2 us
    unnamed x19, local copies, waits for them, and re-layouts  26.9 us
    convert_element_type x2, local copies, waits for them, and re-layouts, update(): (pixel_state.astype(jnp.float32) + change.reshape(pixel_state.shape)).ast...  22.6 us
    dot_general x2, matrix products, predict(): jnp.dot(picker, flat_sums.T, precision=lax.Precision.HIGHEST, preferred_e...  13.3 us
    another operation x6, other arithmetic, solve_mixing(): jnp.linalg.cholesky(jnp.eye(realization_vectors, dtype=jnp.float32) + gram)  13 us
  transfers between devices with their start and end apart: 3, of which 3 were waited for; matrix products, arithmetic and copies ran while one was open for 5% of the time, Pallas kernels for 0%

profile of v1, /device:TPU:8, one launch (start us, length us, event | category | flops | bytes accessed | tf_op | source)
XLA Modules:
  0.0 613.6 jit_solution(8426941856511718304)
XLA Ops:
  11.1 2.3 bitcast_dynamic-update-slice_fusion.5
  24.8 5.1 all-to-all-start
  30.2 2.9 broadcast_multiply_fusion
  33.1 90.9 %all-to-all-done = bf16[8,8,16,4096]{3,2,1,0:T(8,128)(2,1)} async-done(((bf16[8,8,16,4096]{3,2,1,0:T(8,128)(2,1)}), bf16[8,8,16,4096]{3,2,1,0:T(8,128)(2,1)}, u32[]{:S(2)}, u32[]{:S(2)}) %all-to-all-start) | async-done | bytes 8388640 | tf_op jit(solution)/shard_map/all_to_all | solution.py:29
  124.0 4.8 convert_reduce_fusion.1
  128.9 5.8 fusion.9
  134.9 6.6 %convolution_multiply_fusion.1 = f32[1200,64]{0,1:T(8,128)} fusion(f32[1200,1024]{0,1:T(8,128)} %bitcast.114, f32[64,1024]{1,0:T(8,128)S(1)} %reshape_reshape.10), kind=kOutput, calls=%fused_computation.17 | convolution fusion | flops 943795200 | bytes 5484544 | tf_op jit(solution)/shard_map/dot_general | solution.py:47
  142.1 10.9 %convert_bitcast_fusion = (f32[8,8,16,4096]{3,2,1,0:T(8,128)S(1)}, f32[8,8,16,4096]{3,2,1,0:T(8,128)}) fusion(bf16[8,8,16,4096]{3,2,1,0:T(8,128)(2,1)} %all-to-all-done), kind=kLoop, calls=%fused_computation.14 | loop fusion | flops 4194304 | bytes 41943040
  153.0 10.8 %copy.52 = f32[8,8,16,4096]{3,1,2,0:T(8,128)S(1)} copy(f32[8,8,16,4096]{3,2,1,0:T(8,128)S(1)} %get-tuple-element.9) | data formatting | bytes 33554432
  163.8 3.9 subtract_convert_fusion
  167.7 102.2 %all-reduce.3.cloned.1.call-done = f32[1200,64]{0,1:T(8,128)} async-done(((f32[1200,64]{0,1:T(8,128)}), f32[1200,64]{0,1:T(8,128)}) %all-reduce.3.cloned.1.call-update) | async-done | bytes 307216 | tf_op jit(solution)/shard_map/psum | solution.py:121
  272.5 5.8 cholesky.44
  279.6 4.9 custom-call.8
  286.5 21.6 %convert_reduce_fusion = (f32[16,4096]{1,0:T(8,128)S(1)}, bf16[64,16,4096]{2,0,1:T(8,128)(2,1)}) fusion(bf16[64,64,1]{1,0,2:T(8,128)(2,1)S(1)} %fusion.13, bf16[8,16,8,4096]{3,2,1,0:T(8,128)(2,1)} %bitcast.116, f32[8,8,16,4096]{3,2,1,0:T(8,128)} %get-tuple-element.10), kind=kOutput, calls=%fused_computation.2 | convolution fusion | flops 553582592 | bytes 33824768 | tf_op jit(solution)/shard_map/dot_general | solution.py:86
  308.1 11.4 %copy.31 = bf16[64,16,4096]{2,1,0:T(8,128)(2,1)} copy(bf16[64,16,4096]{2,0,1:T(8,128)(2,1)} %get-tuple-element.14) | data formatting | bytes 16777216 | tf_op jit(solution)/shard_map/convert_element_type | solution.py:89
  319.5 5.8 fusion.8
  325.5 6.6 %convolution_multiply_fusion = f32[1200,64]{0,1:T(8,128)} fusion(f32[1200,1024]{0,1:T(8,128)} %bitcast.115, f32[64,1024]{1,0:T(8,128)S(1)} %reshape_reshape.11), kind=kOutput, calls=%fused_computation.16 | convolution fusion | flops 943795200 | bytes 5484544 | tf_op jit(solution)/shard_map/dot_general | solution.py:47
  332.1 128.1 %all-reduce.5.cloned.1.call-done = f32[1200,64]{0,1:T(8,128)} async-done(((f32[1200,64]{0,1:T(8,128)}), f32[1200,64]{0,1:T(8,128)}) %all-reduce.5.cloned.1.call-update) | async-done | bytes 307216 | tf_op jit(solution)/shard_map/psum | solution.py:121
  462.9 5.8 cholesky.55
  470.1 5.0 custom-call.9
  477.1 10.6 %fusion.1 = bf16[64,16,4096]{2,0,1:T(8,128)(2,1)} fusion(bf16[64,16,4096]{2,0,1:T(8,128)(2,1)} %get-tuple-element.14, bf16[64,64,1]{1,0,2:T(8,128)(2,1)S(1)} %fusion.12, f32[16,4096]{1,0:T(8,128)S(1)} %broadcast_multiply_fusion.1), kind=kOutput, calls=%fused_computation.4 | convolution fusion | flops 562036736 | bytes 17047552 | tf_op jit(solution)/shard_map/dot_general | solution.py:86
  487.7 11.2 %copy.38 = bf16[64,16,4096]{2,1,0:T(8,128)(2,1)} copy(bf16[64,16,4096]{2,0,1:T(8,128)(2,1)} %fusion.1) | data formatting | bytes 16777216 | tf_op jit(solution)/shard_map/convert_element_type | solution.py:89
  498.9 99.7 %all_to_all.23 = bf16[64,16,4096]{2,1,0:T(8,128)(2,1)} all-to-all(bf16[64,16,4096]{2,1,0:T(8,128)(2,1)} %copy.38), channel_id=1, replica_groups=mesh['mem'=8,'pix'=4] {'mem'}, dimensions={0} | all-to-all | bytes 16777216 | tf_op jit(solution)/shard_map/all_to_all | solution.py:41
  598.7 7.9 %copy.51 = bf16[8,8,2,8,4096]{4,3,0,2,1:T(8,128)(2,1)} copy(bf16[8,8,2,8,4096]{4,3,2,1,0:T(8,128)(2,1)} %bitcast.117) | data formatting | bytes 16777216 | tf_op jit(solution)/shard_map/all_to_all | solution.py:41
  (54 shorter events, 28.9 us)
Async XLA Ops:
  24.8 5.2 copy-start
  24.8 5.2 copy-start.1
  24.8 5.3 copy-start.2
  24.8 99.1 %all-to-all-start = ((bf16[8,8,16,4096]{3,2,1,0:T(8,128)(2,1)}), bf16[8,8,16,4096]{3,2,1,0:T(8,128)(2,1)}, u32[]{:S(2)}, u32[]{:S(2)}) async-start(bf16[8,8,16,4096]{3,2,1,0:T(8,128)(2,1)} %bitcast_dynamic-update-slice_fusion), calls=%async_computation | async-start | bytes 16777216 | tf_op jit(solution)/shard_map/all_to_all | solution.py:29
  29.9 239.9 %all-reduce.3.cloned.1.call-start = ((), (), s32[]{:S(2)}) async-start(), calls=%async_computation.2 | async-start | bytes 655360 | tf_op jit(solution)/shard_map/psum | solution.py:121
  141.6 318.7 %all-reduce.5.cloned.1.call-start = ((), (), s32[]{:S(2)}) async-start(), calls=%async_computation.3 | async-start | bytes 655360 | tf_op jit(solution)/shard_map/psum | solution.py:121
  163.8 120.7 %copy-start.3 = (f32[2,1200,64]{1,2,0:T(8,128)S(1)}, f32[2,1200,64]{1,2,0:T(8,128)}, u32[]{:S(2)}) copy-start(f32[2,1200,64]{1,2,0:T(8,128)} %param.12) | copy-start | bytes 1843204
  163.8 120.7 %copy-start.4 = (f32[1200]{0:T(1024)S(1)}, f32[1200]{0:T(1024)}, u32[]{:S(2)}) copy-start(f32[1200]{0:T(1024)} %param.10) | copy-start | bytes 14404
Sparse Core Ops, SparseCore 0:
  141.7 128.1 all-reduce.2
  332.2 127.9 all-reduce.4
